TPU v7x, 32 devices: a whole 2x2x4 slice. The times are simulated.
32 devices in a mesh: sp: 16 (over z, y, core), dp: 2 (over x).
Axes of the slice: x: 2, y: 2, z: 4, core: 2. Of those that a mesh axis runs over, the one named last changes fastest.
Arguments:
- query_proj: bfloat16 [4096, 8192], P(('dp', 'sp')), parts along dimension 0, may hold values from -64 to 64
- key_projection: bfloat16 [4096, 1024], P(('dp', 'sp')), parts along dimension 0, may hold values from -64 to 64
- value_projection: bfloat16 [4096, 1024], P(('dp', 'sp')), parts along dimension 0, may hold values from -12 to 12
- query_gain: float32 [128], replicated, may hold values from 1 to 5
- key_norm_gain: float32 [128], replicated, may hold values from 1 to 5
- positions: int32 [4096], P(('dp', 'sp')), parts along dimension 0, may hold values from 0 to 5118, as said below
- doc_start: int32 [4096], P(('dp', 'sp')), parts along dimension 0, may hold values from 0 to 2047, as said below
Outputs:
- attention: bfloat16 [4096, 8192], P(('dp', 'sp')), parts along dimension 0
There are 2 independent parts, one for each index of `dp`. A program takes and returns all parts, laid end to end along the dimension named above; an argument that names none is the same for every part. Nothing has to cross between parts.
Inputs may be any that keep to these rules, and one draw needn't show every extreme that they name: doc_start[i] is the index of the first token of token i's document: it never falls, doc_start[i] <= i < doc_start[i] + 1024, some document has exactly 1024 tokens, and every document but the last has 128 tokens or more. `positions`: within one document the position rises by one from each token to the next.
All inputs are finite; a program needn't handle non-finite values.
Results may differ from a plain program's by a relative error of at most 0.0039.
The roundings to bfloat16 on the way count: a program that leaves them out, or rounds other values in their place, can miss the bound.
Values may be sent and summed in bfloat16 or wider, within the bound.
A program may use at most 64 MiB of HBM per device.

v0:
```python
import jax
import jax.numpy as jnp
from jax import lax
from jax.sharding import PartitionSpec as P

QUERY_HEADS = 64
KEY_VALUE_HEADS = 8
HEAD_SIZE = 128
DOC_MAX = 1024


ROPE_BASE = 1000000.0
NORM_EPS = 1e-06


def from_behind(value, axis, steps):
    count = lax.axis_size(axis)
    leading, last = (max(0, -steps), min(count, count - steps))
    return lax.ppermute(value, axis, [(source, source + steps) for source in range(leading, last)])


def rotary_tables(positions):
    half_dim = HEAD_SIZE // 2
    inv_freq = ROPE_BASE ** (-(jnp.arange(half_dim, dtype=jnp.float32) * 2.0 / HEAD_SIZE))
    angle = positions.astype(jnp.float32)[:, None] * inv_freq[None, :]
    return (jnp.cos(angle), jnp.sin(angle))


def normalize_and_rotate(heads_in, gain, cosine_table, sine_table):
    upcast = heads_in.astype(jnp.float32)
    mean_square = jnp.mean(upcast * upcast, axis=-1, keepdims=True)
    normed = upcast * lax.rsqrt(mean_square + NORM_EPS) * gain
    half_dim = normed.shape[-1] // 2
    first_half = normed[..., :half_dim]
    second_half = normed[..., half_dim:]
    cos_rows = cosine_table[:, None, :]
    sin_rows = sine_table[:, None, :]
    rotated = jnp.concatenate(
        [
            first_half * cos_rows - second_half * sin_rows,
            second_half * cos_rows + first_half * sin_rows,
        ],
        axis=-1,
    )
    return rotated.astype(jnp.bfloat16)


def window_attend(q_rope, k_window, v_window, starts, my_first, window_first):
    device_rows = q_rope.shape[0]
    window_rows = k_window.shape[0]
    head_copies = QUERY_HEADS // KEY_VALUE_HEADS
    scale = HEAD_SIZE ** (-0.5)
    q_grouped = jnp.transpose(
        q_rope.reshape(device_rows, KEY_VALUE_HEADS, head_copies, HEAD_SIZE), (1, 2, 0, 3)
    )
    q_grouped = q_grouped.reshape(KEY_VALUE_HEADS, head_copies * device_rows, HEAD_SIZE)
    k_major = jnp.transpose(k_window, (1, 0, 2))
    v_major = jnp.transpose(v_window, (1, 0, 2))
    row_index = my_first + jnp.arange(device_rows, dtype=jnp.int32)
    key_index = window_first + jnp.arange(window_rows, dtype=jnp.int32)
    visible = (key_index[None, :] >= starts[:, None]) & (key_index[None, :] <= row_index[:, None])

    def one_group(operands):
        query_rows, key_rows, value_rows = operands
        scores = jnp.dot(query_rows, key_rows.T, preferred_element_type=jnp.float32) * scale
        scores = scores.reshape(head_copies, device_rows, window_rows)
        scores = jnp.where(visible[None, :, :], scores, -jnp.inf)
        row_max = jnp.max(scores, axis=2, keepdims=True)
        exp_scores = jnp.exp(scores - row_max)
        row_total = jnp.sum(exp_scores, axis=2, keepdims=True)
        weights = exp_scores.astype(jnp.bfloat16).reshape(head_copies * device_rows, window_rows)
        mixed_out = jnp.dot(weights, value_rows, preferred_element_type=jnp.float32)
        mixed_out = mixed_out.reshape(head_copies, device_rows, HEAD_SIZE) / row_total
        return mixed_out.astype(jnp.bfloat16)

    grouped_out = lax.map(one_group, (q_grouped, k_major, v_major))
    return jnp.transpose(grouped_out, (2, 0, 1, 3)).reshape(device_rows, QUERY_HEADS * HEAD_SIZE)


def body(
    query_proj, key_projection, value_projection, query_gain, key_norm_gain, positions, doc_start
):
    device_rows = query_proj.shape[0]
    cosine_table, sine_table = rotary_tables(positions)
    q_rope = normalize_and_rotate(
        query_proj.reshape(device_rows, QUERY_HEADS, HEAD_SIZE),
        query_gain,
        cosine_table,
        sine_table,
    )
    key_rotated = normalize_and_rotate(
        key_projection.reshape(device_rows, KEY_VALUE_HEADS, HEAD_SIZE),
        key_norm_gain,
        cosine_table,
        sine_table,
    )
    value_head_split = value_projection.reshape(device_rows, KEY_VALUE_HEADS, HEAD_SIZE)
    my_first = lax.axis_index("sp") * device_rows
    reach = (DOC_MAX + device_rows - 1) // device_rows
    own_pair = jnp.stack([key_rotated, value_head_split])
    earlier = []
    for distance in range(reach, 0, -1):
        earlier.append(from_behind(own_pair, "sp", distance))
    window = jnp.concatenate(earlier + [own_pair], axis=1)
    window_first = my_first - reach * device_rows
    return window_attend(q_rope, window[0], window[1], doc_start, my_first, window_first)


def solution(mesh):
    in_specs = (
        P(("dp", "sp"), None),
        P(("dp", "sp"), None),
        P(("dp", "sp"), None),
        P(),
        P(),
        P(("dp", "sp")),
        P(("dp", "sp")),
    )
    out_specs = P(("dp", "sp"), None)
    return jax.shard_map(body, mesh=mesh, in_specs=in_specs, out_specs=out_specs, check_vma=False)
```

profile of v0, /device:TPU:16, one launch (start us, length us, event | category | flops | bytes accessed | tf_op | source)
XLA Modules:
  0.0 189.7 jit_solution(12933578652649027088)
XLA Ops:
  5.6 3.9 %collective-permute-start.1 = (bf16[2,128,8,128]{1,3,2,0:T(8,128)(2,1)S(1)}, bf16[2,128,8,128]{1,3,2,0:T(8,128)(2,1)}, u32[]{:S(2)}, u32[]{:S(2)}) collective-permute-start(bf16[2,128,8,128]{1,3,2,0:T(8,128)(2,1)S(1)} %pad_maximum_fusion.1), channel_id=1, source_target_pairs={{0,14},{2,16},{4,18},{6,20},{8,22},{10,24},{12,26},{14,28},{16,30}... | collective-permute-start | bytes 1572872 | tf_op jit(solution)/shard_map/ppermute | solution.py:19
  9.4 1.9 %collective-permute-start.2 = (bf16[2,128,8,128]{1,3,2,0:T(8,128)(2,1)S(1)}, bf16[2,128,8,128]{1,3,2,0:T(8,128)(2,1)}, u32[]{:S(2)}, u32[]{:S(2)}) collective-permute-start(bf16[2,128,8,128]{1,3,2,0:T(8,128)(2,1)S(1)} %pad_maximum_fusion.1), channel_id=1, source_target_pairs={{0,12},{2,14},{4,16},{6,18},{8,20},{10,22},{12,24},{14,26},{16,28}... | collective-permute-start | bytes 1572872 | tf_op jit(solution)/shard_map/ppermute | solution.py:19
  11.4 1.9 %collective-permute-start.3 = (bf16[2,128,8,128]{1,3,2,0:T(8,128)(2,1)S(1)}, bf16[2,128,8,128]{1,3,2,0:T(8,128)(2,1)}, u32[]{:S(2)}, u32[]{:S(2)}) collective-permute-start(bf16[2,128,8,128]{1,3,2,0:T(8,128)(2,1)S(1)} %pad_maximum_fusion.1), channel_id=1, source_target_pairs={{0,10},{2,12},{4,14},{6,16},{8,18},{10,20},{12,22},{14,24},{16,26}... | collective-permute-start | bytes 1572872 | tf_op jit(solution)/shard_map/ppermute | solution.py:19
  13.3 1.9 %collective-permute-start.4 = (bf16[2,128,8,128]{1,3,2,0:T(8,128)(2,1)S(1)}, bf16[2,128,8,128]{1,3,2,0:T(8,128)(2,1)}, u32[]{:S(2)}, u32[]{:S(2)}) collective-permute-start(bf16[2,128,8,128]{1,3,2,0:T(8,128)(2,1)S(1)} %pad_maximum_fusion.1), channel_id=1, source_target_pairs={{0,8},{2,10},{4,12},{6,14},{8,16},{10,18},{12,20},{14,22},{16,24},... | collective-permute-start | bytes 1572872 | tf_op jit(solution)/shard_map/ppermute | solution.py:19
  23.6 2.5 %pad_maximum_fusion = bf16[128,8,8,128]{3,0,2,1:T(8,128)(2,1)} fusion(bf16[128,8,8,64]{3,0,2,1:T(8,128)(2,1)S(1)} %bitcast.76, bf16[128,8,8,64]{3,0,2,1:T(8,128)(2,1)S(1)} %bitcast.75), kind=kLoop, calls=%fused_computation.27 | loop fusion | flops 4194304 | bytes 4194304 | tf_op jit(solution)/shard_map/concatenate | solution.py:38
  26.1 1.9 %collective-permute-start.5 = (bf16[2,128,8,128]{1,3,2,0:T(8,128)(2,1)S(1)}, bf16[2,128,8,128]{1,3,2,0:T(8,128)(2,1)S(1)}, u32[]{:S(2)}, u32[]{:S(2)}) collective-permute-start(bf16[2,128,8,128]{1,3,2,0:T(8,128)(2,1)S(1)} %pad_maximum_fusion.1), channel_id=1, source_target_pairs={{0,6},{2,8},{4,10},{6,12},{8,14},{10,16},{12,18},{14,20},{16,22},{... | collective-permute-start | bytes 1572872 | tf_op jit(solution)/shard_map/ppermute | solution.py:19
  31.0 14.3 %collective-permute-start.6 = (bf16[2,128,8,128]{1,3,2,0:T(8,128)(2,1)S(1)}, bf16[2,128,8,128]{1,3,2,0:T(8,128)(2,1)S(1)}, u32[]{:S(2)}, u32[]{:S(2)}) collective-permute-start(bf16[2,128,8,128]{1,3,2,0:T(8,128)(2,1)S(1)} %pad_maximum_fusion.1), channel_id=1, source_target_pairs={{0,4},{2,6},{4,8},{6,10},{8,12},{10,14},{12,16},{14,18},{16,20},{1... | collective-permute-start | bytes 1572872 | tf_op jit(solution)/shard_map/ppermute | solution.py:19
  46.4 2.6 %collective-permute-done.2 = bf16[2,128,8,128]{1,3,2,0:T(8,128)(2,1)} collective-permute-done((bf16[2,128,8,128]{1,3,2,0:T(8,128)(2,1)S(1)}, bf16[2,128,8,128]{1,3,2,0:T(8,128)(2,1)}, u32[]{:S(2)}, u32[]{:S(2)}) %collective-permute-start.2) | collective-permute-done | bytes 524320 | tf_op jit(solution)/shard_map/ppermute | solution.py:19
  49.0 22.3 %collective-permute-start.7 = (bf16[2,128,8,128]{1,3,2,0:T(8,128)(2,1)S(1)}, bf16[2,128,8,128]{1,3,2,0:T(8,128)(2,1)S(1)}, u32[]{:S(2)}, u32[]{:S(2)}) collective-permute-start(bf16[2,128,8,128]{1,3,2,0:T(8,128)(2,1)S(1)} %pad_maximum_fusion.1), channel_id=1, source_target_pairs={{0,2},{2,4},{4,6},{6,8},{8,10},{10,12},{12,14},{14,16},{16,18},{18... | collective-permute-start | bytes 1572872 | tf_op jit(solution)/shard_map/ppermute | solution.py:19
  73.7 9.1 %collective-permute-done.4 = bf16[2,128,8,128]{1,3,2,0:T(8,128)(2,1)} collective-permute-done((bf16[2,128,8,128]{1,3,2,0:T(8,128)(2,1)S(1)}, bf16[2,128,8,128]{1,3,2,0:T(8,128)(2,1)}, u32[]{:S(2)}, u32[]{:S(2)}) %collective-permute-start.4) | collective-permute-done | bytes 524320 | tf_op jit(solution)/shard_map/ppermute | solution.py:19
  84.0 4.2 %collective-permute-done.5 = bf16[2,128,8,128]{1,3,2,0:T(8,128)(2,1)S(1)} collective-permute-done((bf16[2,128,8,128]{1,3,2,0:T(8,128)(2,1)S(1)}, bf16[2,128,8,128]{1,3,2,0:T(8,128)(2,1)S(1)}, u32[]{:S(2)}, u32[]{:S(2)}) %collective-permute-start.5) | collective-permute-done | bytes 524320 | tf_op jit(solution)/shard_map/ppermute | solution.py:19
  88.3 40.2 %collective-permute-done.6 = bf16[2,128,8,128]{1,3,2,0:T(8,128)(2,1)S(1)} collective-permute-done((bf16[2,128,8,128]{1,3,2,0:T(8,128)(2,1)S(1)}, bf16[2,128,8,128]{1,3,2,0:T(8,128)(2,1)S(1)}, u32[]{:S(2)}, u32[]{:S(2)}) %collective-permute-start.6) | collective-permute-done | bytes 524320 | tf_op jit(solution)/shard_map/ppermute | solution.py:19
  128.7 5.4 %collective-permute-done.7 = bf16[2,128,8,128]{1,3,2,0:T(8,128)(2,1)S(1)} collective-permute-done((bf16[2,128,8,128]{1,3,2,0:T(8,128)(2,1)S(1)}, bf16[2,128,8,128]{1,3,2,0:T(8,128)(2,1)S(1)}, u32[]{:S(2)}, u32[]{:S(2)}) %collective-permute-start.7) | collective-permute-done | bytes 524320 | tf_op jit(solution)/shard_map/ppermute | solution.py:19
  136.1 47.6 %while.11 = (s32[]{:T(128)}, bf16[8,8,128,128]{3,2,1,0:T(8,128)(2,1)}, bf16[8,1024,128]{2,1,0:T(8,128)(2,1)}, bf16[8,1152,128]{1,2,0:T(8,128)(2,1)S(1)}, bf16[8,...) while((s32[]{:T(128)}, ...), condition=%wide.region_5.6_spmd.clone, body=%wide.region_2.5_spmd.clone.sunk | while | flops 611760128 | bytes 17948252 | solution.py:76
  136.6 2.1 %fusion.29 = (f32[1024]{0:T(1024)S(1)}, f32[1024,1152]{1,0:T(8,128)S(1)}) fusion(pred[1024,1152]{1,0:T(32,128)(4,1)S(1)} %bitcast.72, bf16[8,1152,128]{1,2,0:T(8,128)(2,1)S(1)} %get-tuple-element.173, s32[]{:T(128)} %get-tuple-element.161, bf16[8,1024,128]{2,1,0:T(8,128)(2,1)} %get-tuple-element.172), kind=kOutput, calls=%fused_computation.53.clone.1 | convolution fusion | flops 305527808 | bytes 6460416 | tf_op jit(solution)/shard_map/while/body/eval_jaxpr/dot_general | solution.py:65
  139.6 2.5 %fusion.31 = bf16[8,8,128,128]{3,2,1,0:T(8,128)(2,1)} fusion(bf16[8,8,128,128]{3,2,1,0:T(8,128)(2,1)} %get-tuple-element.162, s32[]{:T(128)} %get-tuple-element.161, bf16[8,128,1152]{2,1,0:T(8,128)(2,1)S(1)} %bitcast.73, bf16[8,1152,128]{1,2,0:T(8,128)(2,1)} %get-tuple-element.174, f32[8,128]{1,0:T(8,128)S(1)} %bitcast.81), kind=kOutput, calls=%fused_computation.9.clone.1 | convolution fusion | flops 302252032 | bytes 2921472 | tf_op jit(solution)/shard_map/while/body/eval_jaxpr/dot_general | solution.py:72
  142.5 2.1 %fusion.29 = (f32[1024]{0:T(1024)S(1)}, f32[1024,1152]{1,0:T(8,128)S(1)}) fusion(pred[1024,1152]{1,0:T(32,128)(4,1)S(1)} %bitcast.72, bf16[8,1152,128]{1,2,0:T(8,128)(2,1)S(1)} %get-tuple-element.173, s32[]{:T(128)} %get-tuple-element.161, bf16[8,1024,128]{2,1,0:T(8,128)(2,1)} %get-tuple-element.172), kind=kOutput, calls=%fused_computation.53.clone.1 | convolution fusion | flops 305527808 | bytes 6460416 | tf_op jit(solution)/shard_map/while/body/eval_jaxpr/dot_general | solution.py:65
  145.5 2.5 %fusion.31 = bf16[8,8,128,128]{3,2,1,0:T(8,128)(2,1)} fusion(bf16[8,8,128,128]{3,2,1,0:T(8,128)(2,1)} %get-tuple-element.162, s32[]{:T(128)} %get-tuple-element.161, bf16[8,128,1152]{2,1,0:T(8,128)(2,1)S(1)} %bitcast.73, bf16[8,1152,128]{1,2,0:T(8,128)(2,1)} %get-tuple-element.174, f32[8,128]{1,0:T(8,128)S(1)} %bitcast.81), kind=kOutput, calls=%fused_computation.9.clone.1 | convolution fusion | flops 302252032 | bytes 2921472 | tf_op jit(solution)/shard_map/while/body/eval_jaxpr/dot_general | solution.py:72
  148.5 2.1 %fusion.29 = (f32[1024]{0:T(1024)S(1)}, f32[1024,1152]{1,0:T(8,128)S(1)}) fusion(pred[1024,1152]{1,0:T(32,128)(4,1)S(1)} %bitcast.72, bf16[8,1152,128]{1,2,0:T(8,128)(2,1)S(1)} %get-tuple-element.173, s32[]{:T(128)} %get-tuple-element.161, bf16[8,1024,128]{2,1,0:T(8,128)(2,1)} %get-tuple-element.172), kind=kOutput, calls=%fused_computation.53.clone.1 | convolution fusion | flops 305527808 | bytes 6460416 | tf_op jit(solution)/shard_map/while/body/eval_jaxpr/dot_general | solution.py:65
  151.5 2.5 %fusion.31 = bf16[8,8,128,128]{3,2,1,0:T(8,128)(2,1)} fusion(bf16[8,8,128,128]{3,2,1,0:T(8,128)(2,1)} %get-tuple-element.162, s32[]{:T(128)} %get-tuple-element.161, bf16[8,128,1152]{2,1,0:T(8,128)(2,1)S(1)} %bitcast.73, bf16[8,1152,128]{1,2,0:T(8,128)(2,1)} %get-tuple-element.174, f32[8,128]{1,0:T(8,128)S(1)} %bitcast.81), kind=kOutput, calls=%fused_computation.9.clone.1 | convolution fusion | flops 302252032 | bytes 2921472 | tf_op jit(solution)/shard_map/while/body/eval_jaxpr/dot_general | solution.py:72
  154.4 2.1 %fusion.29 = (f32[1024]{0:T(1024)S(1)}, f32[1024,1152]{1,0:T(8,128)S(1)}) fusion(pred[1024,1152]{1,0:T(32,128)(4,1)S(1)} %bitcast.72, bf16[8,1152,128]{1,2,0:T(8,128)(2,1)S(1)} %get-tuple-element.173, s32[]{:T(128)} %get-tuple-element.161, bf16[8,1024,128]{2,1,0:T(8,128)(2,1)} %get-tuple-element.172), kind=kOutput, calls=%fused_computation.53.clone.1 | convolution fusion | flops 305527808 | bytes 6460416 | tf_op jit(solution)/shard_map/while/body/eval_jaxpr/dot_general | solution.py:65
  157.4 2.5 %fusion.31 = bf16[8,8,128,128]{3,2,1,0:T(8,128)(2,1)} fusion(bf16[8,8,128,128]{3,2,1,0:T(8,128)(2,1)} %get-tuple-element.162, s32[]{:T(128)} %get-tuple-element.161, bf16[8,128,1152]{2,1,0:T(8,128)(2,1)S(1)} %bitcast.73, bf16[8,1152,128]{1,2,0:T(8,128)(2,1)} %get-tuple-element.174, f32[8,128]{1,0:T(8,128)S(1)} %bitcast.81), kind=kOutput, calls=%fused_computation.9.clone.1 | convolution fusion | flops 302252032 | bytes 2921472 | tf_op jit(solution)/shard_map/while/body/eval_jaxpr/dot_general | solution.py:72
  160.4 2.1 %fusion.29 = (f32[1024]{0:T(1024)S(1)}, f32[1024,1152]{1,0:T(8,128)S(1)}) fusion(pred[1024,1152]{1,0:T(32,128)(4,1)S(1)} %bitcast.72, bf16[8,1152,128]{1,2,0:T(8,128)(2,1)S(1)} %get-tuple-element.173, s32[]{:T(128)} %get-tuple-element.161, bf16[8,1024,128]{2,1,0:T(8,128)(2,1)} %get-tuple-element.172), kind=kOutput, calls=%fused_computation.53.clone.1 | convolution fusion | flops 305527808 | bytes 6460416 | tf_op jit(solution)/shard_map/while/body/eval_jaxpr/dot_general | solution.py:65
  163.4 2.5 %fusion.31 = bf16[8,8,128,128]{3,2,1,0:T(8,128)(2,1)} fusion(bf16[8,8,128,128]{3,2,1,0:T(8,128)(2,1)} %get-tuple-element.162, s32[]{:T(128)} %get-tuple-element.161, bf16[8,128,1152]{2,1,0:T(8,128)(2,1)S(1)} %bitcast.73, bf16[8,1152,128]{1,2,0:T(8,128)(2,1)} %get-tuple-element.174, f32[8,128]{1,0:T(8,128)S(1)} %bitcast.81), kind=kOutput, calls=%fused_computation.9.clone.1 | convolution fusion | flops 302252032 | bytes 2921472 | tf_op jit(solution)/shard_map/while/body/eval_jaxpr/dot_general | solution.py:72
  166.3 2.1 %fusion.29 = (f32[1024]{0:T(1024)S(1)}, f32[1024,1152]{1,0:T(8,128)S(1)}) fusion(pred[1024,1152]{1,0:T(32,128)(4,1)S(1)} %bitcast.72, bf16[8,1152,128]{1,2,0:T(8,128)(2,1)S(1)} %get-tuple-element.173, s32[]{:T(128)} %get-tuple-element.161, bf16[8,1024,128]{2,1,0:T(8,128)(2,1)} %get-tuple-element.172), kind=kOutput, calls=%fused_computation.53.clone.1 | convolution fusion | flops 305527808 | bytes 6460416 | tf_op jit(solution)/shard_map/while/body/eval_jaxpr/dot_general | solution.py:65
  169.3 2.5 %fusion.31 = bf16[8,8,128,128]{3,2,1,0:T(8,128)(2,1)} fusion(bf16[8,8,128,128]{3,2,1,0:T(8,128)(2,1)} %get-tuple-element.162, s32[]{:T(128)} %get-tuple-element.161, bf16[8,128,1152]{2,1,0:T(8,128)(2,1)S(1)} %bitcast.73, bf16[8,1152,128]{1,2,0:T(8,128)(2,1)} %get-tuple-element.174, f32[8,128]{1,0:T(8,128)S(1)} %bitcast.81), kind=kOutput, calls=%fused_computation.9.clone.1 | convolution fusion | flops 302252032 | bytes 2921472 | tf_op jit(solution)/shard_map/while/body/eval_jaxpr/dot_general | solution.py:72
  172.3 2.1 %fusion.29 = (f32[1024]{0:T(1024)S(1)}, f32[1024,1152]{1,0:T(8,128)S(1)}) fusion(pred[1024,1152]{1,0:T(32,128)(4,1)S(1)} %bitcast.72, bf16[8,1152,128]{1,2,0:T(8,128)(2,1)S(1)} %get-tuple-element.173, s32[]{:T(128)} %get-tuple-element.161, bf16[8,1024,128]{2,1,0:T(8,128)(2,1)} %get-tuple-element.172), kind=kOutput, calls=%fused_computation.53.clone.1 | convolution fusion | flops 305527808 | bytes 6460416 | tf_op jit(solution)/shard_map/while/body/eval_jaxpr/dot_general | solution.py:65
  175.3 2.5 %fusion.31 = bf16[8,8,128,128]{3,2,1,0:T(8,128)(2,1)} fusion(bf16[8,8,128,128]{3,2,1,0:T(8,128)(2,1)} %get-tuple-element.162, s32[]{:T(128)} %get-tuple-element.161, bf16[8,128,1152]{2,1,0:T(8,128)(2,1)S(1)} %bitcast.73, bf16[8,1152,128]{1,2,0:T(8,128)(2,1)} %get-tuple-element.174, f32[8,128]{1,0:T(8,128)S(1)} %bitcast.81), kind=kOutput, calls=%fused_computation.9.clone.1 | convolution fusion | flops 302252032 | bytes 2921472 | tf_op jit(solution)/shard_map/while/body/eval_jaxpr/dot_general | solution.py:72
  178.2 2.1 %fusion.29 = (f32[1024]{0:T(1024)S(1)}, f32[1024,1152]{1,0:T(8,128)S(1)}) fusion(pred[1024,1152]{1,0:T(32,128)(4,1)S(1)} %bitcast.72, bf16[8,1152,128]{1,2,0:T(8,128)(2,1)S(1)} %get-tuple-element.173, s32[]{:T(128)} %get-tuple-element.161, bf16[8,1024,128]{2,1,0:T(8,128)(2,1)} %get-tuple-element.172), kind=kOutput, calls=%fused_computation.53.clone.1 | convolution fusion | flops 305527808 | bytes 6460416 | tf_op jit(solution)/shard_map/while/body/eval_jaxpr/dot_general | solution.py:65
  181.2 2.5 %fusion.31 = bf16[8,8,128,128]{3,2,1,0:T(8,128)(2,1)} fusion(bf16[8,8,128,128]{3,2,1,0:T(8,128)(2,1)} %get-tuple-element.162, s32[]{:T(128)} %get-tuple-element.161, bf16[8,128,1152]{2,1,0:T(8,128)(2,1)S(1)} %bitcast.73, bf16[8,1152,128]{1,2,0:T(8,128)(2,1)} %get-tuple-element.174, f32[8,128]{1,0:T(8,128)S(1)} %bitcast.81), kind=kOutput, calls=%fused_computation.9.clone.1 | convolution fusion | flops 302252032 | bytes 2921472 | tf_op jit(solution)/shard_map/while/body/eval_jaxpr/dot_general | solution.py:72
  183.7 2.9 %copy.19 = bf16[128,8,8,128]{3,2,1,0:T(8,128)(2,1)S(1)} copy(bf16[128,8,8,128]{3,0,2,1:T(8,128)(2,1)} %bitcast.13) | data formatting | bytes 4194304 | tf_op jit(solution)/shard_map/transpose | solution.py:77
  186.6 3.1 %copy.25 = bf16[16,8,64,128]{3,1,2,0:T(8,128)(2,1)} copy(bf16[16,8,64,128]{3,2,1,0:T(8,128)(2,1)S(1)} %bitcast.77) | data formatting | bytes 4194304
  (67 shorter events, 35.0 us)
Async XLA Ops:
  0.0 15.4 %copy-start = (bf16[128,8192]{1,0:T(8,128)(2,1)S(1)}, bf16[128,8192]{1,0:T(8,128)(2,1)}, u32[]{:S(2)}) copy-start(bf16[128,8192]{1,0:T(8,128)(2,1)} %param.9) | copy-start | bytes 6291460
  4.3 21.9 %collective-permute-start = (bf16[2,128,8,128]{1,3,2,0:T(8,128)(2,1)S(1)}, bf16[2,128,8,128]{1,3,2,0:T(8,128)(2,1)}, u32[]{:S(2)}, u32[]{:S(2)}) collective-permute-start(bf16[2,128,8,128]{1,3,2,0:T(8,128)(2,1)S(1)} %pad_maximum_fusion.1), channel_id=1, source_target_pairs={{0,16},{2,18},{4,20},{6,22},{8,24},{10,26},{12,28},{14,30},{1,17},... | collective-permute-start | bytes 1572872 | tf_op jit(solution)/shard_map/ppermute | solution.py:19
  5.6 25.4 %collective-permute-start.1 = (bf16[2,128,8,128]{1,3,2,0:T(8,128)(2,1)S(1)}, bf16[2,128,8,128]{1,3,2,0:T(8,128)(2,1)}, u32[]{:S(2)}, u32[]{:S(2)}) collective-permute-start(bf16[2,128,8,128]{1,3,2,0:T(8,128)(2,1)S(1)} %pad_maximum_fusion.1), channel_id=1, source_target_pairs={{0,14},{2,16},{4,18},{6,20},{8,22},{10,24},{12,26},{14,28},{16,30}... | collective-permute-start | bytes 1572872 | tf_op jit(solution)/shard_map/ppermute | solution.py:19
  9.4 39.6 %collective-permute-start.2 = (bf16[2,128,8,128]{1,3,2,0:T(8,128)(2,1)S(1)}, bf16[2,128,8,128]{1,3,2,0:T(8,128)(2,1)}, u32[]{:S(2)}, u32[]{:S(2)}) collective-permute-start(bf16[2,128,8,128]{1,3,2,0:T(8,128)(2,1)S(1)} %pad_maximum_fusion.1), channel_id=1, source_target_pairs={{0,12},{2,14},{4,16},{6,18},{8,20},{10,22},{12,24},{14,26},{16,28}... | collective-permute-start | bytes 1572872 | tf_op jit(solution)/shard_map/ppermute | solution.py:19
  11.4 61.1 %collective-permute-start.3 = (bf16[2,128,8,128]{1,3,2,0:T(8,128)(2,1)S(1)}, bf16[2,128,8,128]{1,3,2,0:T(8,128)(2,1)}, u32[]{:S(2)}, u32[]{:S(2)}) collective-permute-start(bf16[2,128,8,128]{1,3,2,0:T(8,128)(2,1)S(1)} %pad_maximum_fusion.1), channel_id=1, source_target_pairs={{0,10},{2,12},{4,14},{6,16},{8,18},{10,20},{12,22},{14,24},{16,26}... | collective-permute-start | bytes 1572872 | tf_op jit(solution)/shard_map/ppermute | solution.py:19
  13.3 69.5 %collective-permute-start.4 = (bf16[2,128,8,128]{1,3,2,0:T(8,128)(2,1)S(1)}, bf16[2,128,8,128]{1,3,2,0:T(8,128)(2,1)}, u32[]{:S(2)}, u32[]{:S(2)}) collective-permute-start(bf16[2,128,8,128]{1,3,2,0:T(8,128)(2,1)S(1)} %pad_maximum_fusion.1), channel_id=1, source_target_pairs={{0,8},{2,10},{4,12},{6,14},{8,16},{10,18},{12,20},{14,22},{16,24},... | collective-permute-start | bytes 1572872 | tf_op jit(solution)/shard_map/ppermute | solution.py:19
  16.6 1.2 copy-start.2
  26.1 62.1 %collective-permute-start.5 = (bf16[2,128,8,128]{1,3,2,0:T(8,128)(2,1)S(1)}, bf16[2,128,8,128]{1,3,2,0:T(8,128)(2,1)S(1)}, u32[]{:S(2)}, u32[]{:S(2)}) collective-permute-start(bf16[2,128,8,128]{1,3,2,0:T(8,128)(2,1)S(1)} %pad_maximum_fusion.1), channel_id=1, source_target_pairs={{0,6},{2,8},{4,10},{6,12},{8,14},{10,16},{12,18},{14,20},{16,22},{... | collective-permute-start | bytes 1572872 | tf_op jit(solution)/shard_map/ppermute | solution.py:19
  31.0 97.6 %collective-permute-start.6 = (bf16[2,128,8,128]{1,3,2,0:T(8,128)(2,1)S(1)}, bf16[2,128,8,128]{1,3,2,0:T(8,128)(2,1)S(1)}, u32[]{:S(2)}, u32[]{:S(2)}) collective-permute-start(bf16[2,128,8,128]{1,3,2,0:T(8,128)(2,1)S(1)} %pad_maximum_fusion.1), channel_id=1, source_target_pairs={{0,4},{2,6},{4,8},{6,10},{8,12},{10,14},{12,16},{14,18},{16,20},{1... | collective-permute-start | bytes 1572872 | tf_op jit(solution)/shard_map/ppermute | solution.py:19
  49.0 85.1 %collective-permute-start.7 = (bf16[2,128,8,128]{1,3,2,0:T(8,128)(2,1)S(1)}, bf16[2,128,8,128]{1,3,2,0:T(8,128)(2,1)S(1)}, u32[]{:S(2)}, u32[]{:S(2)}) collective-permute-start(bf16[2,128,8,128]{1,3,2,0:T(8,128)(2,1)S(1)} %pad_maximum_fusion.1), channel_id=1, source_target_pairs={{0,2},{2,4},{4,6},{6,8},{8,10},{10,12},{12,14},{14,16},{16,18},{18... | collective-permute-start | bytes 1572872 | tf_op jit(solution)/shard_map/ppermute | solution.py:19
  134.3 1.8 copy-start.1
where the time goes:
time: 191 us; the launch traced here: 190 us
  waiting for transfers between devices  63.3 us (33%)
  starting transfers between devices  49.4 us (26%)
  matrix products  36.1 us (19%)
  local copies, waits for them, and re-layouts  22.5 us (12%)
  other arithmetic  18 us (9%)
    ppermute x8, waiting for transfers between devices, from_behind(): lax.ppermute(value, axis, [(source, source + steps) for source in range(l...  63.3 us
    ppermute x8, starting transfers between devices, from_behind(): lax.ppermute(value, axis, [(source, source + steps) for source in range(l...  49.4 us
    dot_general x8, matrix products, one_group(): mixed_out = jnp.dot(weights, value_rows, preferred_element_type=jnp.float32)  19.6 us
    dot_general x8, matrix products, one_group(): jnp.dot(query_rows, key_rows.T, preferred_element_type=jnp.float32) * scale  16.5 us
    unnamed x18, local copies, waits for them, and re-layouts  12.5 us
    reduce_sum x8, other arithmetic, one_group(): row_total = jnp.sum(exp_scores, axis=2, keepdims=True)  7.4 us
  transfers between devices with their start and end apart: 8, of which 6 were waited for; matrix products, arithmetic and copies ran while one was open for 9% of the time, Pallas kernels for 0%

commit v1 on v0

v1 whole, which is shorter than its diff:
```python
import functools
import math

import jax
import jax.numpy as jnp
import numpy as np
from jax import lax
from jax.experimental import pallas as pl
from jax.experimental.pallas import tpu as pltpu
from jax.sharding import PartitionSpec as P

HEAD_SIZE = 128
DOC_MAX = 1024
REACH = 8
ROPE_BASE = 1000000.0
NORM_EPS = 1e-06
HIDDEN = -1e30
Q_TILE = 2
MESH = pl.DeviceIdType.MESH

OWN_Z, OWN_Y, OWN_C, F4_Z, F4_Y, F4_C, F8_Y, F8_C, F2_C, F6_C = range(10)


def norm_rope(block, gain, cos_full, sin_full):
    up = block.astype(jnp.float32)
    mean_square = jnp.mean(up * up, axis=-1, keepdims=True)
    normed = up * lax.rsqrt(mean_square + NORM_EPS) * gain
    swapped = pltpu.roll(normed, HEAD_SIZE // 2, axis=1)
    return (normed * cos_full + swapped * sin_full).astype(jnp.bfloat16)


def kernel(
    count, groups, copies, rows,
    q_hbm, k_hbm, v_hbm, qg_hbm, kg_hbm, freq_hbm, pos_hbm, start_hbm,
    o_ref, win, hidden, q_ref, k_ref, q_rope, qg_ref, kg_ref, freq_ref, pos_ref, start_ref,
    local_sem, in_sem, send_sem, recv_sem,
):
    me = lax.axis_index("sp")
    core = lax.rem(me, 2)
    side = lax.rem(lax.div(me, 2), 2)
    core_peer = me + 1 - 2 * core
    side_peer = me + 2 - 4 * side
    window = (REACH + 1) * rows

    def slot_rows(slot):
        return pl.ds(pl.multiple_of((REACH - slot) * rows, rows), rows)

    def send(kind, g, source, target_slot, target):
        return pltpu.make_async_remote_copy(
            src_ref=win.at[g, :, slot_rows(source)],
            dst_ref=win.at[g, :, slot_rows(target_slot)],
            send_sem=send_sem.at[kind, g],
            recv_sem=recv_sem.at[target_slot, g],
            device_id={"sp": target},
            device_id_type=MESH,
        )

    has_next = me + 4 < count
    f4_slot = 6 - 4 * side

    plan = {
        OWN_Z: (has_next, 0, 4, me + 4),
        OWN_Y: (side == 0, 0, 2, side_peer),
        OWN_C: (core == 0, 0, 1, core_peer),
        F4_Z: ((me >= 4) & has_next, 4, 8, me + 4),
        F4_Y: (me >= 4, 4, f4_slot, side_peer),
        F4_C: (me >= 4, 4, 5 - 2 * core, core_peer),
        F8_Y: ((me >= 8) & (side == 1), 8, 6, side_peer),
        F8_C: ((me >= 8) & (core == 1), 8, 7, core_peer),
        F2_C: (me >= 2, 2, 3 - 2 * core, core_peer),
        F6_C: (me >= 6, 6, 7 - 2 * core, core_peer),
    }

    def start(kind, g):
        condition, source, target_slot, target = plan[kind]

        @pl.when(condition)
        def _():
            send(kind, g, source, target_slot, target).start()

    def arrived(slot, g):
        @pl.when(me >= slot)
        def _():
            send(OWN_Z, g, 0, slot, me).wait_recv()

    value_copies = [
        pltpu.make_async_copy(
            v_hbm.at[:, pl.ds(g * HEAD_SIZE, HEAD_SIZE)],
            win.at[g, 1, pl.ds(REACH * rows, rows)],
            local_sem.at[g],
        )
        for g in range(groups)
    ]
    small = [
        pltpu.make_async_copy(source, target, in_sem.at[i])
        for i, (source, target) in enumerate([
            (k_hbm, k_ref), (kg_hbm, kg_ref), (freq_hbm, freq_ref), (pos_hbm, pos_ref),
            (start_hbm, start_ref), (qg_hbm, qg_ref),
        ])
    ]
    query_copy = pltpu.make_async_copy(q_hbm, q_ref, in_sem.at[6])
    for copy in small + value_copies + [query_copy]:
        copy.start()
    barrier = pltpu.get_barrier_semaphore()
    for peer in (core_peer, side_peer):
        pl.semaphore_signal(barrier, inc=1, device_id={"sp": peer}, device_id_type=MESH)

    @pl.when(has_next)
    def _():
        pl.semaphore_signal(barrier, inc=1, device_id={"sp": me + 4}, device_id_type=MESH)

    @pl.when(me >= 4)
    def _():
        pl.semaphore_signal(barrier, inc=1, device_id={"sp": me - 4}, device_id_type=MESH)

    for copy in small:
        copy.wait()
    places = jnp.broadcast_to(pos_ref[...].astype(jnp.float32), (HEAD_SIZE, rows)).T
    angle = places * freq_ref[...]
    lane = lax.broadcasted_iota(jnp.int32, (rows, HEAD_SIZE), 1)
    cos_full = jnp.cos(angle)
    sine = jnp.sin(angle)
    sin_full = jnp.where(lane < HEAD_SIZE // 2, -sine, sine)
    for g in range(groups):
        win[g, 0, pl.ds(REACH * rows, rows), :] = norm_rope(
            k_ref[:, g * HEAD_SIZE:(g + 1) * HEAD_SIZE], kg_ref[...], cos_full, sin_full
        )

    token = me * rows + lax.broadcasted_iota(jnp.int32, (window, rows), 1)
    key_index = (me - REACH) * rows + lax.broadcasted_iota(jnp.int32, (window, rows), 0)
    visible = (key_index >= start_ref[...]) & (key_index <= token)
    hidden[...] = jnp.where(visible, 0.0, HIDDEN).astype(jnp.bfloat16)

    @pl.loop(0, jnp.maximum(REACH - me, 0))
    def _(j):
        for g in range(groups):
            win[g, :, pl.ds(pl.multiple_of(j * rows, rows), rows), :] = jnp.zeros(
                (2, rows, HEAD_SIZE), jnp.bfloat16
            )

    for copy in value_copies:
        copy.wait()
    inner = (me >= 4) & has_next

    @pl.when(inner)
    def _():
        pl.semaphore_wait(barrier, 4)

    @pl.when(jnp.logical_not(inner))
    def _():
        pl.semaphore_wait(barrier, 3 if count > 4 else 2)

    scale = HEAD_SIZE ** (-0.5) * math.log2(math.e)

    unit = (
        lax.broadcasted_iota(jnp.int32, (rows, rows), 0)
        == lax.broadcasted_iota(jnp.int32, (rows, rows), 1)
    ).astype(jnp.bfloat16)
    units = jnp.concatenate([unit] * Q_TILE, axis=0)

    def columns(g, head):
        return pl.ds(pl.multiple_of((g * copies + head) * HEAD_SIZE, HEAD_SIZE), HEAD_SIZE)

    def attend(g):
        keys = jnp.concatenate([win[g, 0], hidden[...]], axis=1)
        values = jnp.concatenate(
            [win[g, 1], jnp.ones((window, HEAD_SIZE), jnp.bfloat16)], axis=1
        )
        for first in range(0, copies, Q_TILE):
            queries = jnp.concatenate(
                [q_rope[g, first * rows:(first + Q_TILE) * rows], units], axis=1
            )
            scores = lax.dot_general(
                queries, keys, (((1,), (1,)), ((), ())), preferred_element_type=jnp.float32
            )
            row_max = jnp.max(scores, axis=1, keepdims=True)
            weights = jnp.exp2((scores - row_max) * scale).astype(jnp.bfloat16)
            mixed = jnp.dot(weights, values, preferred_element_type=jnp.float32)
            mixed = mixed[:, :HEAD_SIZE] / mixed[:, HEAD_SIZE:]
            for r in range(Q_TILE):
                o_ref[:, columns(g, first + r)] = mixed[r * rows:(r + 1) * rows].astype(
                    jnp.bfloat16
                )

    LEAD = 4
    for g in range(min(LEAD, groups)):
        for kind in (OWN_Z, OWN_Y, OWN_C):
            start(kind, g)

    query_copy.wait()

    @pl.loop(0, groups)
    def _(g):
        for head in range(copies):
            q_rope[g, head * rows:(head + 1) * rows] = norm_rope(
                q_ref[:, columns(g, head)], qg_ref[...], cos_full, sin_full
            )

    @pl.loop(0, groups + 3)
    def _(tick):
        @pl.when(tick + LEAD < groups)
        def _():
            for kind in (OWN_Z, OWN_Y, OWN_C):
                start(kind, tick + LEAD)

        @pl.when(tick < groups)
        def _():
            arrived(4, tick)
            for kind in (F4_Z, F4_Y, F4_C):
                start(kind, tick)

        @pl.when((tick >= 1) & (tick < groups + 1))
        def _():
            arrived(8, tick - 1)
            for kind in (F8_Y, F8_C):
                start(kind, tick - 1)
            arrived(2, tick - 1)
            start(F2_C, tick - 1)

        @pl.when((tick >= 2) & (tick < groups + 2))
        def _():
            arrived(6, tick - 2)
            start(F6_C, tick - 2)

        @pl.when(tick >= 3)
        def _():
            for slot in (1, 3, 5, 7):
                arrived(slot, tick - 3)
            attend(tick - 3)

    @pl.loop(0, groups)
    def _(g):
        for kind, (condition, source, target_slot, target) in plan.items():
            @pl.when(condition)
            def _():
                send(kind, g, source, target_slot, target).wait_send()


def solution(mesh):
    count = mesh.shape["sp"]

    def body(query_proj, key_projection, value_projection, query_gain, key_norm_gain, positions, doc_start):
        rows = query_proj.shape[0]
        groups = key_projection.shape[1] // HEAD_SIZE
        copies = query_proj.shape[1] // key_projection.shape[1]
        assert rows * REACH >= DOC_MAX and count % 4 == 0
        half_dim = HEAD_SIZE // 2
        inv_freq = ROPE_BASE ** (-(np.arange(half_dim) * 2.0 / HEAD_SIZE))
        freq = jnp.asarray(np.concatenate([inv_freq, inv_freq])[None, :], jnp.float32)
        window = (REACH + 1) * rows
        return pl.pallas_call(
            functools.partial(kernel, count, groups, copies, rows),
            out_shape=jax.ShapeDtypeStruct(query_proj.shape, jnp.bfloat16),
            in_specs=[pl.BlockSpec(memory_space=pl.ANY)] * 8,
            out_specs=pl.BlockSpec(memory_space=pltpu.VMEM),
            scratch_shapes=[
                pltpu.VMEM((groups, 2, window, HEAD_SIZE), jnp.bfloat16),
                pltpu.VMEM((window, rows), jnp.bfloat16),
                pltpu.VMEM(query_proj.shape, jnp.bfloat16),
                pltpu.VMEM(key_projection.shape, jnp.bfloat16),
                pltpu.VMEM((groups, copies * rows, HEAD_SIZE), jnp.bfloat16),
                pltpu.VMEM((1, HEAD_SIZE), jnp.float32),
                pltpu.VMEM((1, HEAD_SIZE), jnp.float32),
                pltpu.VMEM((1, HEAD_SIZE), jnp.float32),
                pltpu.VMEM((1, rows), jnp.int32),
                pltpu.VMEM((1, rows), jnp.int32),
                pltpu.SemaphoreType.DMA((groups,)),
                pltpu.SemaphoreType.DMA((7,)),
                pltpu.SemaphoreType.DMA((10, groups)),
                pltpu.SemaphoreType.DMA((REACH + 1, groups)),
            ],
            compiler_params=pltpu.CompilerParams(
                collective_id=0, has_side_effects=True, vmem_limit_bytes=60 * 1024 * 1024
            ),
        )(
            query_proj, key_projection, value_projection,
            query_gain[None, :], key_norm_gain[None, :], freq, positions[None, :], doc_start[None, :],
        )

    tokens = P(("dp", "sp"), None)
    vector = P(("dp", "sp"))
    return jax.shard_map(
        body,
        mesh=mesh,
        in_specs=(tokens, tokens, tokens, P(), P(), vector, vector),
        out_specs=tokens,
        check_vma=False,
    )
```

time: 191 us -> 47.6 us (0.25)
  waiting for transfers between devices: 63.3 us -> 0 us
  starting transfers between devices: 49.4 us -> 0 us
  Pallas kernels: 0 us -> 44.3 us
  matrix products: 36.1 us -> 0 us
  local copies, waits for them, and re-layouts: 22.5 us -> 3.1 us
  other arithmetic: 18 us -> 0 us
    ppermute x8 -> x0, waiting for transfers between devices: 63.3 us -> none  [from_behind(): lax.ppermute(value, axis, [(source, source + steps) for source in range(l...]
    ppermute x8 -> x0, starting transfers between devices: 49.4 us -> none  [from_behind(): lax.ppermute(value, axis, [(source, source + steps) for source in range(l...]
    pallas_call x0 -> x1, Pallas kernels: none -> 44.3 us  [body(): pl.pallas_call(functools.partial(kernel, count, groups, copies, rows), ou...]
    dot_general x16 -> x0, matrix products: 36.1 us -> none  [the longest x8 19.6 us: one_group(): mixed_out = jnp.dot(weights, value_rows, preferred_element_type=jnp.float32)]
    unnamed x18 -> x1, local copies, waits for them, and re-layouts: 12.5 us -> 3.1 us
    reduce_sum x10 -> x0, other arithmetic: 8.62 us -> none  [the longest x8 7.4 us: one_group(): row_total = jnp.sum(exp_scores, axis=2, keepdims=True)]
    transpose x2 -> x0, local copies, waits for them, and re-layouts: 4.7 us -> none  [the longest x1 2.94 us: window_attend(): jnp.transpose(grouped_out, (2, 0, 1, 3))]
    another operation x2 -> x0, local copies, waits for them, and re-layouts: 2.71 us -> none
  transfers between devices with their start and end apart: 8 -> 0, of which waited for: 6 -> 0; matrix products, arithmetic and copies ran while one was open for 9% -> 0% of each run, Pallas kernels for 0% -> 0%
where the time goes in v1:
time: 47.6 us; the launch traced here: 47.4 us
  Pallas kernels  44.3 us (93%)
  local copies, waits for them, and re-layouts  3.1 us (7%)
    pallas_call x1, Pallas kernels, body(): pl.pallas_call(functools.partial(kernel, count, groups, copies, rows), ou...  44.3 us
    unnamed x1, local copies, waits for them, and re-layouts  3.1 us

profile of v1, /device:TPU:16, one launch (start us, length us, event | category | flops | bytes accessed | tf_op | source)
XLA Modules:
  0.0 47.4 jit_solution(15209182783846770319)
XLA Ops:
  0.0 44.3 %shard_map.82 = bf16[128,8192]{1,0:T(8,128)(2,1)} custom-call(bf16[128,8192]{1,0:T(8,128)(2,1)} %q_hbm.1, bf16[128,1024]{1,0:T(8,128)(2,1)} %k_hbm.1, bf16[128,1024]{1,0:T(8,128)(2,1)} %v_hbm.1, f32[1,128]{1,0:T(1,128)} %bitcast.4, f32[1,128]{1,0:T(1,128)} %bitcast.5, f32[1,128]{1,0:T(1,128)} %constant.2.clone.freq_hbm, s32[1,128]{1,0:T(1,128)} %bitcast.6, ...), custom_call_target="tpu_custom_call" | custom-call | tf_op jit(solution)/shard_map/pallas_call | solution.py:251
  44.3 3.1 %copy.10 = bf16[128,8192]{1,0:T(8,128)(2,1)} copy(bf16[128,8192]{1,0:T(8,128)(2,1)} %shard_map.82) | data formatting | bytes 4194304
